TPU v7x, 32 devices: a whole 2x2x4 slice. The times are simulated.
32 devices in a mesh: row: 4 (over x, core), col: 8 (over z, y).
Axes of the slice: x: 2, y: 2, z: 4, core: 2. Of those that a mesh axis runs over, the one named last changes fastest.
Arguments:
- tiles: int32 [4, 8, 8, 128, 128], P('row', 'col'), may hold values from 0 to 1073741823, as said below
- slots: int32 [4, 8, 8], P('row', 'col'), may hold values from 0 to 31, as said below
- factor: float32 [4096, 256], P(('row', 'col')), may hold values from -0.5 to 0.5
- dual: float32 [4096, 256], P(('row', 'col')), may hold values from -0.5 to 0.5
Outputs:
- final_factor: float32 [4096, 256], P(('row', 'col'))
- final_dual: float32 [4096, 256], P(('row', 'col'))
- objective: float32 [3], replicated
- residual: float32 [3], replicated
Inputs may be any that keep to these rules, and one draw needn't show every extreme that they name: `slots`: for every device, 8 distinct block numbers in ascending order. The stored blocks of all devices form a symmetric pattern: the block of rows piece p and columns piece q is stored if and only if the block of rows piece q and columns piece p is; every diagonal block is stored. `tiles`: the stored block of rows piece p and columns piece q is the transpose of the one of rows piece q and columns piece p; diagonal blocks are symmetric.
All inputs are finite; a program needn't handle non-finite values.
Results may differ from a plain program's by a relative error of at most 0.005.
Values may be sent and summed in bfloat16 or wider, within the bound.
A program may use at most 64 MiB of HBM per device.

v0:
```python
import math
import jax
import jax.numpy as jnp
from jax import lax
from jax.sharding import PartitionSpec as P

ITERS = 3
penalty = 2.0
step_size = 0.25
ridge_shift = 0.1
offset = 536870912


def block_weights(integers, vertices):
    unit_scale = math.sqrt(6.0 / vertices) / 2.0**29
    return ((integers - offset).astype(jnp.float32) * unit_scale).astype(jnp.bfloat16)


def unit_rows(values):
    return values * lax.rsqrt(jnp.sum(values * values, axis=1, keepdims=True) + 1e-06)


def local(tiles, slots, factor, dual):
    row_count = lax.axis_size("row")
    col_count = lax.axis_size("col")
    piece_rows = factor.shape[0]
    columns = factor.shape[1]
    vertices = piece_rows * row_count * col_count
    weights = block_weights(tiles.reshape(tiles.shape[2], piece_rows, piece_rows), vertices)
    stored = slots.reshape(-1)
    block_row = stored // row_count
    block_col = stored % row_count

    def combine(partial_value):
        return lax.psum_scatter(partial_value, "col", scatter_dimension=0, tiled=True)

    selector = (block_row[None, :] == jnp.arange(col_count, dtype=jnp.int32)[:, None]).astype(
        jnp.float32
    )
    block_sums = jnp.sum(weights, axis=2, dtype=jnp.float32)
    edge_sums = jnp.dot(selector, block_sums, precision=lax.Precision.HIGHEST)
    degree = combine(edge_sums.reshape(-1))
    current = factor
    lagrange = dual
    projected = unit_rows(current + lagrange / penalty)
    tallies = []
    for iteration in range(ITERS):
        packed = current.astype(jnp.bfloat16)
        own_gram = lax.dot_general(
            packed, packed, (((0,), (0,)), ((), ())), preferred_element_type=jnp.float32
        )
        gram_total = lax.psum(own_gram, ("row", "col"))
        gathered = lax.all_gather(packed, "row", axis=0, tiled=True).reshape(
            -1, piece_rows, columns
        )
        chosen = gathered[block_col]
        products = jnp.einsum("tij,tjk->tik", weights, chosen, preferred_element_type=jnp.float32)
        partial_value = jnp.einsum(
            "at,tik->aik", selector, products, precision=lax.Precision.HIGHEST
        )
        coupled = combine(partial_value.reshape(col_count * piece_rows, columns))
        widened = packed.astype(jnp.float32)
        gradient = degree[:, None] * widened - coupled
        precond = columns / vertices * gram_total + ridge_shift * jnp.eye(
            columns, dtype=jnp.float32
        )
        triangle = jnp.linalg.cholesky(precond)
        descent = 2.0 * gradient - lagrange - penalty * (current - projected)
        current = current + step_size * jax.scipy.linalg.cho_solve((triangle, True), descent.T).T
        projected = unit_rows(current + lagrange / penalty)
        lagrange = lagrange + penalty * (current - projected)
        mismatch = current - projected
        local_sums = jnp.stack([jnp.sum(widened * gradient), jnp.sum(mismatch * mismatch)])
        tallies.append(local_sums)
    stacked = jnp.stack(tallies)
    stacked = lax.psum(stacked, ("row", "col"))
    objective = stacked[:, 0] / (4.0 * vertices)
    residual = stacked[:, 1] / vertices
    return (current, lagrange, objective, residual)


def solution(mesh):
    in_specs = (
        P("row", "col", None, None, None),
        P("row", "col", None),
        P(("row", "col"), None),
        P(("row", "col"), None),
    )
    out_specs = (P(("row", "col"), None), P(("row", "col"), None), P(), P())
    return jax.shard_map(local, mesh=mesh, in_specs=in_specs, out_specs=out_specs, check_vma=False)
```

profile of v0, /device:TPU:0, one launch (start us, length us, event | category | flops | bytes accessed | tf_op | source)
XLA Modules:
  0.0 669.2 jit_solution(12461409791366380685)
XLA Ops:
  10.2 7.2 %all_gather.9 = bf16[512,256]{0,1:T(8,128)(2,1)S(1)} all-gather(bf16[128,256]{0,1:T(8,128)(2,1)S(1)} %get-tuple-element.92), channel_id=1, replica_groups=mesh['row'=4,'col'=8] {'row'}, dimensions={0}, use_global_device_ids=true | all-gather | bytes 327680 | tf_op jit(solution)/shard_map/all_gather | solution.py:53
  21.8 22.3 %all-reduce.1 = f32[1024]{0:T(1024)S(1)} all-reduce(f32[1024]{0:T(1024)S(1)} %convolution_bitcast_fusion), channel_id=2, replica_groups=mesh['row'=4,'col'=8] {'col'}, use_global_device_ids=true, to_apply=%region_6.8.clone | all-reduce | flops 1024 | bytes 8192
  46.1 99.0 %all-reduce.6.cloned.1.call-done = f32[256,256]{0,1:T(8,128)} async-done(((f32[256,256]{0,1:T(8,128)}), f32[256,256]{0,1:T(8,128)}) %all-reduce.6.cloned.1.call-update) | async-done | bytes 262160 | tf_op jit(solution)/shard_map/psum | solution.py:52
  147.1 11.7 %cholesky.172 = f32[128,128]{1,0:T(8,128)S(1)} custom-call(f32[128,128]{1,0:T(8,128)S(1)} %cholesky.270), custom_call_target="Cholesky" | custom-call | tf_op jit(solution)/shard_map/jit(cholesky)/cholesky | solution.py:67
  158.9 9.8 %custom-call.17 = f32[1,128,128]{1,2,0:T(8,128)S(1)} custom-call(f32[1,128,128]{2,1,0:T(8,128)S(1)} %get-tuple-element.104), custom_call_target="InvertDiagBlocksLowerTriangular" | custom-call | tf_op jit(solution)/shard_map/jit(cholesky)/cholesky | solution.py:67
  169.2 11.7 %cholesky.189 = f32[128,128]{1,0:T(8,128)S(1)} custom-call(f32[128,128]{1,0:T(8,128)S(1)} %convolution_subtract_fusion.8), custom_call_target="Cholesky" | custom-call | tf_op jit(solution)/shard_map/jit(cholesky)/cholesky | solution.py:67
  183.0 4.2 while.6
  187.2 19.7 %custom-call.18 = f32[2,128,128]{1,2,0:T(8,128)S(1)} custom-call(f32[2,128,128]{2,1,0:T(8,128)S(1)} %get-tuple-element.26), custom_call_target="InvertDiagBlocksLowerTriangular" | custom-call | tf_op jit(solution)/shard_map/jit(_cho_solve)/triangular_solve | solution.py:69
  209.4 5.8 all_gather.10
  220.1 126.6 %all-reduce.8.cloned.1.call-done = f32[256,256]{0,1:T(8,128)} async-done(((f32[256,256]{0,1:T(8,128)}), f32[256,256]{0,1:T(8,128)}) %all-reduce.8.cloned.1.call-update) | async-done | bytes 262160 | tf_op jit(solution)/shard_map/psum | solution.py:52
  348.7 11.7 %cholesky.206 = f32[128,128]{1,0:T(8,128)S(1)} custom-call(f32[128,128]{1,0:T(8,128)S(1)} %cholesky.273), custom_call_target="Cholesky" | custom-call | tf_op jit(solution)/shard_map/jit(cholesky)/cholesky | solution.py:67
  360.4 9.8 %custom-call.19 = f32[1,128,128]{1,2,0:T(8,128)S(1)} custom-call(f32[1,128,128]{2,1,0:T(8,128)S(1)} %get-tuple-element.100), custom_call_target="InvertDiagBlocksLowerTriangular" | custom-call | tf_op jit(solution)/shard_map/jit(cholesky)/cholesky | solution.py:67
  370.7 11.7 %cholesky.223 = f32[128,128]{1,0:T(8,128)S(1)} custom-call(f32[128,128]{1,0:T(8,128)S(1)} %convolution_subtract_fusion.5), custom_call_target="Cholesky" | custom-call | tf_op jit(solution)/shard_map/jit(cholesky)/cholesky | solution.py:67
  385.1 4.2 while.7
  389.3 19.7 %custom-call.20 = f32[2,128,128]{1,2,0:T(8,128)S(1)} custom-call(f32[2,128,128]{2,1,0:T(8,128)S(1)} %get-tuple-element.27), custom_call_target="InvertDiagBlocksLowerTriangular" | custom-call | tf_op jit(solution)/shard_map/jit(_cho_solve)/triangular_solve | solution.py:69
  413.1 5.8 all_gather.11
  422.7 126.8 %all-reduce.10.cloned.1.call-done = f32[256,256]{0,1:T(8,128)} async-done(((f32[256,256]{0,1:T(8,128)}), f32[256,256]{0,1:T(8,128)}) %all-reduce.10.cloned.1.call-update) | async-done | bytes 262160 | tf_op jit(solution)/shard_map/psum | solution.py:52
  551.5 11.7 %cholesky.240 = f32[128,128]{1,0:T(8,128)S(1)} custom-call(f32[128,128]{1,0:T(8,128)S(1)} %cholesky.276), custom_call_target="Cholesky" | custom-call | tf_op jit(solution)/shard_map/jit(cholesky)/cholesky | solution.py:67
  563.3 9.8 %custom-call.21 = f32[1,128,128]{1,2,0:T(8,128)S(1)} custom-call(f32[1,128,128]{2,1,0:T(8,128)S(1)} %get-tuple-element.96), custom_call_target="InvertDiagBlocksLowerTriangular" | custom-call | tf_op jit(solution)/shard_map/jit(cholesky)/cholesky | solution.py:67
  573.6 11.7 %cholesky.257 = f32[128,128]{1,0:T(8,128)S(1)} custom-call(f32[128,128]{1,0:T(8,128)S(1)} %convolution_subtract_fusion.2), custom_call_target="Cholesky" | custom-call | tf_op jit(solution)/shard_map/jit(cholesky)/cholesky | solution.py:67
  588.0 4.3 while.8
  592.3 19.7 %custom-call.22 = f32[2,128,128]{1,2,0:T(8,128)S(1)} custom-call(f32[2,128,128]{2,1,0:T(8,128)S(1)} %get-tuple-element.28), custom_call_target="InvertDiagBlocksLowerTriangular" | custom-call | tf_op jit(solution)/shard_map/jit(_cho_solve)/triangular_solve | solution.py:69
  612.0 1.7 fusion.7
  621.5 39.2 %psum.31 = f32[3,2]{1,0:T(4,128)S(1)} all-reduce(f32[3,2]{1,0:T(4,128)S(1)} %pad_maximum_fusion), channel_id=1, replica_groups=mesh['row'=4,'col'=8] {'row','col'}, use_global_device_ids=true, to_apply=%region_22.25 | all-reduce | flops 6 | bytes 48 | tf_op jit(solution)/shard_map/psum | solution.py:76
  (159 shorter events, 54.2 us)
Async XLA Ops:
  8.0 1.1 copy-start.6
  8.0 137.1 %all-reduce.6.cloned.1.call-start = ((), (), s32[]{:S(2)}) async-start(), calls=%async_computation.3 | async-start | bytes 524288 | tf_op jit(solution)/shard_map/psum | solution.py:52
  9.2 8.3 %copy-start.4 = (s32[1,1,8,128,128]{4,3,2,1,0:T(8,128)S(1)}, s32[1,1,8,128,128]{4,3,2,1,0:T(8,128)}, u32[]{:S(2)}) copy-start(s32[1,1,8,128,128]{4,3,2,1,0:T(8,128)} %param.7) | copy-start | bytes 1572868
  10.2 7.3 %copy-start.7 = (s32[1,1,8]{2,1,0:T(1,128)S(1)}, s32[1,1,8]{2,1,0:T(1,128)}, u32[]{:S(2)}) copy-start(s32[1,1,8]{2,1,0:T(1,128)} %param.8) | copy-start | bytes 100
  10.2 196.7 %reduce-scatter.4.cloned.1.call-start = ((), (), s32[]{:S(2)}) async-start(), calls=%async_computation.4 | async-start | bytes 1179648 | tf_op jit(solution)/shard_map/reduce_scatter | solution.py:35
  21.6 325.0 %all-reduce.8.cloned.1.call-start = ((), (), s32[]{:S(2)}) async-start(), calls=%async_computation.5 | async-start | bytes 524288 | tf_op jit(solution)/shard_map/psum | solution.py:52
  44.1 0.7 copy-start.8
  146.1 1.0 copy-start
  219.4 189.6 %reduce-scatter.6.cloned.1.call-start = ((), (), s32[]{:S(2)}) async-start(), calls=%async_computation.6 | async-start | bytes 1179648 | tf_op jit(solution)/shard_map/reduce_scatter | solution.py:35
  220.0 329.5 %all-reduce.10.cloned.1.call-start = ((), (), s32[]{:S(2)}) async-start(), calls=%async_computation.7 | async-start | bytes 524288 | tf_op jit(solution)/shard_map/psum | solution.py:52
  347.6 1.0 copy-start.1
  422.2 189.8 %reduce-scatter.8.cloned.1.call-start = ((), (), s32[]{:S(2)}) async-start(), calls=%async_computation.8 | async-start | bytes 1179648 | tf_op jit(solution)/shard_map/reduce_scatter | solution.py:35
  550.5 1.0 copy-start.2
  587.9 24.1 %copy-start.5 = (f32[128,256]{0,1:T(8,128)S(1)}, f32[128,256]{0,1:T(8,128)}, u32[]{:S(2)}) copy-start(f32[128,256]{0,1:T(8,128)} %reduce-scatter.4.cloned.1.call-done) | copy-start | bytes 393220
  588.0 24.0 %copy-start.3 = (f32[128,256]{0,1:T(8,128)S(1)}, f32[128,256]{0,1:T(8,128)}, u32[]{:S(2)}) copy-start(f32[128,256]{0,1:T(8,128)} %reduce-scatter.6.cloned.1.call-done) | copy-start | bytes 393220
Sparse Core Ops, SparseCore 0:
  14.3 130.7 all-reduce.5
  219.5 127.0 all-reduce.7
  422.3 127.1 all-reduce.9
Sparse Core Ops, SparseCore 1:
  21.7 66.1 reduce-scatter.3
  223.3 63.7 reduce-scatter.5
  426.0 63.8 reduce-scatter.7
where the time goes:
time: 673 us; the launch traced here: 669 us
  waiting for transfers between devices  354 us (53%)
  other arithmetic  176 us (26%)
  blocking collectives  80.4 us (12%)
  local copies, waits for them, and re-layouts  25.8 us (4%)
  between operations  21.1 us (3%)
  matrix products  11.9 us (2%)
    psum x3, waiting for transfers between devices, local(): gram_total = lax.psum(own_gram, ('row', 'col'))  352 us
    another operation x20, other arithmetic, local(): triangle = jnp.linalg.cholesky(precond)  103 us
    another operation x7, other arithmetic, local(): jax.scipy.linalg.cho_solve((triangle, True), descent.T)  59.1 us
    psum x1, blocking collectives, local(): stacked = lax.psum(stacked, ('row', 'col'))  39.2 us
    unnamed x1, blocking collectives  22.3 us
    all_gather x3, blocking collectives, local(): lax.all_gather(packed, 'row', axis=0, tiled=True)  18.8 us
  transfers between devices with their start and end apart: 6, of which 3 were waited for; matrix products, arithmetic and copies ran while one was open for 27% of the time, Pallas kernels for 0%

commit v1 on v0

--- a/solution.py
+++ b/solution.py
@@ -9,6 +9,12 @@
 step_size = 0.25
 ridge_shift = 0.1
 offset = 536870912
+
+
+def add_all(shard, axis):
+    terms = lax.all_gather(shard, axis, axis=0, tiled=False)
+    result = terms.sum(axis=0)
+    return result
 
 
 def block_weights(integers, vertices):
@@ -49,7 +55,7 @@
         own_gram = lax.dot_general(
             packed, packed, (((0,), (0,)), ((), ())), preferred_element_type=jnp.float32
         )
-        gram_total = lax.psum(own_gram, ("row", "col"))
+        gram_total = add_all(own_gram, ("row", "col"))
         gathered = lax.all_gather(packed, "row", axis=0, tiled=True).reshape(
             -1, piece_rows, columns
         )

time: 673 us -> 559 us (0.83)
  waiting for transfers between devices: 354 us -> 231 us
  other arithmetic: 176 us -> 187 us
    psum x3 -> x0, waiting for transfers between devices: 352 us -> none  [local(): gram_total = lax.psum(own_gram, ('row', 'col'))]
    reduce_scatter x3, waiting for transfers between devices: 0.08 us -> 231 us  [combine(): lax.psum_scatter(partial_value, 'col', scatter_dimension=0, tiled=True)]
    reduce_sum x0 -> x3, other arithmetic: none -> 11.8 us  [add_all(): result = terms.sum(axis=0)]
  transfers between devices with their start and end apart: 6 -> 6, of which waited for: 3 -> 3; matrix products, arithmetic and copies ran while one was open for 27% -> 2% of each run, Pallas kernels for 0% -> 0%
where the time goes in v1:
time: 559 us; the launch traced here: 555 us
  waiting for transfers between devices  231 us (41%)
  other arithmetic  187 us (33%)
  blocking collectives  79.3 us (14%)
  local copies, waits for them, and re-layouts  24.3 us (4%)
  between operations  20.9 us (4%)
  matrix products  11.8 us (2%)
    reduce_scatter x3, waiting for transfers between devices, combine(): lax.psum_scatter(partial_value, 'col', scatter_dimension=0, tiled=True)  231 us
    another operation x20, other arithmetic, local(): triangle = jnp.linalg.cholesky(precond)  103 us
    another operation x7, other arithmetic, local(): jax.scipy.linalg.cho_solve((triangle, True), descent.T)  59.1 us
    psum x1, blocking collectives, local(): stacked = lax.psum(stacked, ('row', 'col'))  38 us
    unnamed x1, blocking collectives  22.4 us
    all_gather x3, blocking collectives, local(): lax.all_gather(packed, 'row', axis=0, tiled=True)  18.9 us
    another operation x22, local copies, waits for them, and re-layouts, local(): jax.scipy.linalg.cho_solve((triangle, True), descent.T)  12.1 us
    reduce_sum x3, other arithmetic, add_all(): result = terms.sum(axis=0)  11.8 us
  transfers between devices with their start and end apart: 6, of which 3 were waited for; matrix products, arithmetic and copies ran while one was open for 2% of the time, Pallas kernels for 0%

profile of v1, /device:TPU:0, one launch (start us, length us, event | category | flops | bytes accessed | tf_op | source)
XLA Modules:
  0.0 555.5 jit_solution(6155257905949352195)
XLA Ops:
  11.4 7.2 %all_gather.29 = bf16[512,256]{0,1:T(8,128)(2,1)S(1)} all-gather(bf16[128,256]{0,1:T(8,128)(2,1)S(1)} %get-tuple-element.92), channel_id=1, replica_groups=mesh['row'=4,'col'=8] {'row'}, dimensions={0}, use_global_device_ids=true | all-gather | bytes 327680 | tf_op jit(solution)/shard_map/all_gather | solution.py:59
  26.3 22.4 %all-reduce.1 = f32[1024]{0:T(1024)S(1)} all-reduce(f32[1024]{0:T(1024)S(1)} %convolution_bitcast_fusion), channel_id=5, replica_groups=mesh['row'=4,'col'=8] {'col'}, use_global_device_ids=true, to_apply=%region_6.8.clone | all-reduce | flops 1024 | bytes 8192
  48.8 62.7 %reduce-scatter.4.cloned.1.call-done = f32[128,256]{0,1:T(8,128)} async-done(((f32[1024,256]{0,1:T(8,128)}), f32[128,256]{0,1:T(8,128)}) %reduce-scatter.4.cloned.1.call-update) | async-done | bytes 131088 | tf_op jit(solution)/shard_map/reduce_scatter | solution.py:41
  112.5 3.9 reduce_sum.126
  116.8 11.7 %cholesky.172 = f32[128,128]{1,0:T(8,128)S(1)} custom-call(f32[128,128]{1,0:T(8,128)S(1)} %cholesky.270), custom_call_target="Cholesky" | custom-call | tf_op jit(solution)/shard_map/jit(cholesky)/cholesky | solution.py:73
  128.6 9.8 %custom-call.17 = f32[1,128,128]{1,2,0:T(8,128)S(1)} custom-call(f32[1,128,128]{2,1,0:T(8,128)S(1)} %get-tuple-element.104), custom_call_target="InvertDiagBlocksLowerTriangular" | custom-call | tf_op jit(solution)/shard_map/jit(cholesky)/cholesky | solution.py:73
  138.9 11.7 %cholesky.189 = f32[128,128]{1,0:T(8,128)S(1)} custom-call(f32[128,128]{1,0:T(8,128)S(1)} %convolution_subtract_fusion.8), custom_call_target="Cholesky" | custom-call | tf_op jit(solution)/shard_map/jit(cholesky)/cholesky | solution.py:73
  152.7 4.2 while.6
  156.9 19.7 %custom-call.18 = f32[2,128,128]{1,2,0:T(8,128)S(1)} custom-call(f32[2,128,128]{2,1,0:T(8,128)S(1)} %get-tuple-element.26), custom_call_target="InvertDiagBlocksLowerTriangular" | custom-call | tf_op jit(solution)/shard_map/jit(_cho_solve)/triangular_solve | solution.py:75
  178.1 5.9 %all_gather.32 = bf16[512,256]{0,1:T(8,128)(2,1)S(1)} all-gather(bf16[128,256]{0,1:T(8,128)(2,1)S(1)} %get-tuple-element.78), channel_id=1, replica_groups=mesh['row'=4,'col'=8] {'row'}, dimensions={0}, use_global_device_ids=true | all-gather | bytes 327680 | tf_op jit(solution)/shard_map/all_gather | solution.py:59
  188.4 84.3 %reduce-scatter.6.cloned.1.call-done = f32[128,256]{0,1:T(8,128)} async-done(((f32[1024,256]{0,1:T(8,128)}), f32[128,256]{0,1:T(8,128)}) %reduce-scatter.6.cloned.1.call-update) | async-done | bytes 131088 | tf_op jit(solution)/shard_map/reduce_scatter | solution.py:41
  278.6 11.7 %cholesky.206 = f32[128,128]{1,0:T(8,128)S(1)} custom-call(f32[128,128]{1,0:T(8,128)S(1)} %cholesky.273), custom_call_target="Cholesky" | custom-call | tf_op jit(solution)/shard_map/jit(cholesky)/cholesky | solution.py:73
  290.4 9.8 %custom-call.19 = f32[1,128,128]{1,2,0:T(8,128)S(1)} custom-call(f32[1,128,128]{2,1,0:T(8,128)S(1)} %get-tuple-element.100), custom_call_target="InvertDiagBlocksLowerTriangular" | custom-call | tf_op jit(solution)/shard_map/jit(cholesky)/cholesky | solution.py:73
  300.7 11.7 %cholesky.223 = f32[128,128]{1,0:T(8,128)S(1)} custom-call(f32[128,128]{1,0:T(8,128)S(1)} %convolution_subtract_fusion.5), custom_call_target="Cholesky" | custom-call | tf_op jit(solution)/shard_map/jit(cholesky)/cholesky | solution.py:73
  315.2 4.5 while.7
  319.7 19.7 %custom-call.20 = f32[2,128,128]{1,2,0:T(8,128)S(1)} custom-call(f32[2,128,128]{2,1,0:T(8,128)S(1)} %get-tuple-element.27), custom_call_target="InvertDiagBlocksLowerTriangular" | custom-call | tf_op jit(solution)/shard_map/jit(_cho_solve)/triangular_solve | solution.py:75
  340.9 5.8 %all_gather.35 = bf16[512,256]{0,1:T(8,128)(2,1)S(1)} all-gather(bf16[128,256]{0,1:T(8,128)(2,1)S(1)} %convert_element_type.43), channel_id=1, replica_groups=mesh['row'=4,'col'=8] {'row'}, dimensions={0}, use_global_device_ids=true | all-gather | bytes 327680 | tf_op jit(solution)/shard_map/all_gather | solution.py:59
  351.1 84.0 %reduce-scatter.8.cloned.1.call-done = f32[128,256]{0,1:T(8,128)} async-done(((f32[1024,256]{0,1:T(8,128)}), f32[128,256]{0,1:T(8,128)}) %reduce-scatter.8.cloned.1.call-update) | async-done | bytes 131088 | tf_op jit(solution)/shard_map/reduce_scatter | solution.py:41
  442.4 11.7 %cholesky.240 = f32[128,128]{1,0:T(8,128)S(1)} custom-call(f32[128,128]{1,0:T(8,128)S(1)} %cholesky.276), custom_call_target="Cholesky" | custom-call | tf_op jit(solution)/shard_map/jit(cholesky)/cholesky | solution.py:73
  454.2 9.8 %custom-call.21 = f32[1,128,128]{1,2,0:T(8,128)S(1)} custom-call(f32[1,128,128]{2,1,0:T(8,128)S(1)} %get-tuple-element.96), custom_call_target="InvertDiagBlocksLowerTriangular" | custom-call | tf_op jit(solution)/shard_map/jit(cholesky)/cholesky | solution.py:73
  464.5 11.7 %cholesky.257 = f32[128,128]{1,0:T(8,128)S(1)} custom-call(f32[128,128]{1,0:T(8,128)S(1)} %convolution_subtract_fusion.2), custom_call_target="Cholesky" | custom-call | tf_op jit(solution)/shard_map/jit(cholesky)/cholesky | solution.py:73
  478.9 4.2 while.8
  483.0 19.7 %custom-call.22 = f32[2,128,128]{1,2,0:T(8,128)S(1)} custom-call(f32[2,128,128]{2,1,0:T(8,128)S(1)} %get-tuple-element.28), custom_call_target="InvertDiagBlocksLowerTriangular" | custom-call | tf_op jit(solution)/shard_map/jit(_cho_solve)/triangular_solve | solution.py:75
  508.5 38.0 %psum.7 = f32[3,2]{1,0:T(4,128)S(1)} all-reduce(f32[3,2]{1,0:T(4,128)S(1)} %pad_maximum_fusion), channel_id=1, replica_groups=mesh['row'=4,'col'=8] {'row','col'}, use_global_device_ids=true, to_apply=%region_22.25 | all-reduce | flops 6 | bytes 48 | tf_op jit(solution)/shard_map/psum | solution.py:82
  (153 shorter events, 60.8 us)
Async XLA Ops:
  8.0 17.0 %copy-start.2 = (u32[32]{0:T(128)S(1)}, u32[32]{0:T(128)}, u32[]{:S(2)}) copy-start(u32[32]{0:T(128)} %constant.153) | copy-start | bytes 388
  8.0 103.5 %reduce-scatter.4.cloned.1.call-start = ((), (), s32[]{:S(2)}) async-start(), calls=%async_computation.3 | async-start | bytes 1179648 | tf_op jit(solution)/shard_map/reduce_scatter | solution.py:41
  23.9 88.6 %all-gather.7.cloned.1.call-start = ((), (), s32[]{:S(2)}) async-start(), calls=%async_computation.6 | async-start | bytes 8650752 | tf_op jit(solution)/shard_map/all_gather | solution.py:15
  24.9 247.8 %reduce-scatter.6.cloned.1.call-start = ((), (), s32[]{:S(2)}) async-start(), calls=%async_computation.4 | async-start | bytes 1179648 | tf_op jit(solution)/shard_map/reduce_scatter | solution.py:41
  187.3 87.0 %all-gather.9.cloned.1.call-start = ((), (), s32[]{:S(2)}) async-start(), calls=%async_computation.7 | async-start | bytes 8650752 | tf_op jit(solution)/shard_map/all_gather | solution.py:15
  188.3 246.8 %reduce-scatter.8.cloned.1.call-start = ((), (), s32[]{:S(2)}) async-start(), calls=%async_computation.5 | async-start | bytes 1179648 | tf_op jit(solution)/shard_map/reduce_scatter | solution.py:41
  278.5 156.5 %copy-start = (f32[128,256]{0,1:T(8,128)S(1)}, f32[128,256]{0,1:T(8,128)}, u32[]{:S(2)}) copy-start(f32[128,256]{0,1:T(8,128)} %reduce-scatter.6.cloned.1.call-done) | copy-start | bytes 393220
  278.6 156.5 %copy-start.1 = (f32[128,256]{0,1:T(8,128)S(1)}, f32[128,256]{0,1:T(8,128)}, u32[]{:S(2)}) copy-start(f32[128,256]{0,1:T(8,128)} %reduce-scatter.4.cloned.1.call-done) | copy-start | bytes 393220
  350.1 88.0 %all-gather.11.cloned.1.call-start = ((), (), s32[]{:S(2)}) async-start(), calls=%async_computation.8 | async-start | bytes 8650752 | tf_op jit(solution)/shard_map/all_gather | solution.py:15
Sparse Core Ops, SparseCore 0:
  24.0 87.4 reduce-scatter.3
  187.4 85.2 reduce-scatter.5
  350.2 84.7 reduce-scatter.7
Sparse Core Ops, SparseCore 1:
  27.4 80.0 all-gather.6
  190.8 77.8 all-gather.8
  353.6 77.7 all-gather.10
